TPU v7x, 32 devices: a whole 2x2x4 slice. The times are simulated.
32 devices in a mesh: energy: 16 (over z, x, core), space: 2 (over y).
Axes of the slice: x: 2, y: 2, z: 4, core: 2. Of those that a mesh axis runs over, the one named last changes fastest.
Arguments:
- g_lesser: float32 [2, 256, 2, 256, 256], P(None, 'energy', 'space'), may hold values from -6 to 6
- g_greater: float32 [2, 256, 2, 256, 256], P(None, 'energy', 'space'), may hold values from -6 to 6
- v_diag: float32 [2, 256, 256], P('space'), may hold values from -0.375 to 0.375
- v_upper: float32 [2, 256, 256], P('space'), may hold values from -0.375 to 0.375
Outputs:
- screened: float32 [2, 64, 2, 256, 256], P(None, 'energy', 'space')
All inputs are finite; a program needn't handle non-finite values.
Results may differ from a plain program's by a relative error of at most 0.000098.
Values sent between devices are 32-bit elements; how exact they have to be, the bound alone decides.
A program may use at most 128 MiB of HBM per device.

v0:
```python
import functools
import math

import jax
import jax.numpy as jnp
import numpy as np
from jax import lax
from jax.experimental import pallas as pl
from jax.experimental.pallas import tpu as pltpu
from jax.sharding import PartitionSpec as P

NW = 64
PREFACTOR = 0.0625
ROWS = 8
HIGH = lax.Precision.HIGH


def split_np(table):
    table = np.asarray(table, np.float64)
    high = table.astype(jnp.bfloat16)
    low = (table - high.astype(np.float64)).astype(jnp.bfloat16)
    return np.concatenate([high, low, high], axis=1)


def tables(keep):
    length = 2 * keep

    def forward(start, sign):
        phase = 2.0 * math.pi / length * (np.outer(np.arange(length), np.arange(start, start + keep)) % length)
        cos, sin = np.cos(phase), sign * np.sin(phase)
        return np.block([[cos, sin], [-sin, cos]])

    phase = 2.0 * math.pi / length * (np.outer(np.arange(keep), np.arange(length)) % length)
    cos, sin = np.cos(phase) * (PREFACTOR / length), np.sin(phase) * (PREFACTOR / length)
    back = np.block([[cos, -sin], [sin, cos]])
    wide = [np.concatenate([forward(0, sign), forward(keep, sign)], axis=1) for sign in (1, -1)]
    narrow = [forward(0, sign) for sign in (1, -1)]
    return [jnp.asarray(split_np(t)) for t in (*wide, *narrow, back)]


def stacked(value):
    high = value.astype(jnp.bfloat16)
    low = (value - high.astype(jnp.float32)).astype(jnp.bfloat16)
    return jnp.concatenate([high, high, low], axis=0)


def dot(table, value):
    return jnp.dot(table, stacked(value), preferred_element_type=jnp.float32)


def correlate_kernel(
    n, group, rows, less_wide, great_wide, less_narrow, great_narrow, back_tab, less, great, out, near,
    less_buf, great_buf, halo_buf, polar_buf, parts_buf, total_buf,
    in_send, in_recv, own_sem, halo_send, halo_recv, out_send, out_recv, out_own, near_send, near_recv,
):
    me = lax.axis_index("energy")
    mine, share = me // group, lax.rem(me, group)
    groups = n // group
    sources, buffers = (less, great), (less_buf, great_buf)
    held = less.shape[1]
    kept = out.shape[1]
    row = lax.axis_index("space")
    sides = near.shape[0]
    stages = less_buf.shape[0]
    keep = polar_buf.shape[2]
    half = less_buf.shape[4] // 2
    mesh_id = pl.DeviceIdType.MESH

    def in_copy(k, q, d):
        other = lax.rem(share + d, group)
        return pltpu.make_async_remote_copy(
            src_ref=sources[k].at[:, :, other, q],
            dst_ref=buffers[k].at[q, :, pl.ds(share * held, held)],
            send_sem=in_send.at[k, q, d],
            recv_sem=in_recv.at[k, q, d],
            device_id={"energy": mine * group + other},
            device_id_type=mesh_id,
        )

    def in_own(k, q):
        return pltpu.make_async_copy(
            sources[k].at[:, :, share, q], buffers[k].at[q, :, pl.ds(share * held, held)], own_sem.at[k, q]
        )

    def halo_copy(k, q):
        lanes = pl.ds((1 - k) * half, half)
        peer = lax.rem(me + (group if k else n - group), n)
        return pltpu.make_async_remote_copy(
            src_ref=buffers[k].at[q, :, :, :, lanes],
            dst_ref=halo_buf.at[q, :, :, :, lanes],
            send_sem=halo_send.at[k, q],
            recv_sem=halo_recv.at[k, q],
            device_id={"energy": peer},
            device_id_type=mesh_id,
        )

    sends = (mine > 0, mine < groups - 1)
    receives = (mine < groups - 1, mine > 0)

    def out_copy(q, d):
        peer = lax.rem(me + d, n)
        return pltpu.make_async_remote_copy(
            src_ref=polar_buf.at[q, :, pl.ds(peer * kept, kept)],
            dst_ref=parts_buf.at[q, mine, :, :, share],
            send_sem=out_send.at[q, d],
            recv_sem=out_recv.at[q, d],
            device_id={"energy": peer},
            device_id_type=mesh_id,
        )

    def out_mine(q):
        return pltpu.make_async_copy(total_buf.at[q], out.at[:, :, :, q], out_own.at[q])

    def near_copy(side, q):
        return pltpu.make_async_remote_copy(
            src_ref=total_buf.at[q],
            dst_ref=near.at[side, :, :, :, q],
            send_sem=near_send.at[side, q],
            recv_sem=near_recv.at[side, q],
            device_id={"space": lax.rem(row + (rows - 1 if side else 1), rows)},
            device_id_type=mesh_id,
        )

    def near_if(side, receiving, body):
        if rows == 2:
            body()
        else:
            pl.when(row > 0 if side != receiving else row < rows - 1)(body)

    def each(first, last, body):
        def step(d, carry):
            body(d)
            return carry
        lax.fori_loop(first, last, step, 0)

    barrier = pltpu.get_barrier_semaphore()
    each(1, n, lambda d: pl.semaphore_signal(
        barrier, inc=1, device_id={"energy": lax.rem(me + d, n)}, device_id_type=mesh_id))
    for side in range(sides):
        pl.semaphore_signal(
            barrier, inc=1, device_id={"space": lax.rem(row + (rows - 1 if side else 1), rows)}, device_id_type=mesh_id)
    pl.semaphore_wait(barrier, n - 1 + sides)

    def send_stage(q):
        for k in range(2):
            in_own(k, q).start()
            each(1, group, lambda d: in_copy(k, q, d).start())

    each(0, stages, send_stage)

    def forward_stage(q):
        for k in range(2):
            in_own(k, q).wait()
            each(1, group, lambda d: in_copy(k, q, d).wait_recv())

            @pl.when(sends[k])
            def _():
                halo_copy(k, q).start()

    def pair(buf, q, i, j):
        lanes = slice(j * half, (j + 1) * half)
        return jnp.concatenate([buf[q, :, :, i + s, lanes].reshape(2 * keep, half) for s in range(2)], axis=1)

    def compute_stage(q):
        for k in range(2):
            @pl.when(receives[k])
            def _():
                halo_copy(k, q).wait_recv()

            @pl.when(jnp.logical_not(receives[k]))
            def _():
                lanes = slice((1 - k) * half, (2 - k) * half)
                halo_buf[q, :, :, :, lanes] = jnp.zeros((2, keep, ROWS, half), jnp.float32)

        for i in range(0, ROWS, 2):
            for j in range(2):
                less_x, great_x = pair(less_buf, q, i, j), pair(great_buf, q, i, j)
                halo_x = pair(halo_buf, q, i, j)
                if j == 0:
                    spec_l = dot(less_narrow[...], less_x)
                    spec_g = dot(great_wide[...], jnp.concatenate([great_x, halo_x], axis=0))
                else:
                    spec_l = dot(less_wide[...], jnp.concatenate([less_x, halo_x], axis=0))
                    spec_g = dot(great_narrow[...], great_x)
                mid = spec_l.shape[0] // 2
                lr, li, gr, gi = spec_l[:mid], spec_l[mid:], spec_g[:mid], spec_g[mid:]
                spec = jnp.concatenate([lr * gr - li * gi, lr * gi + li * gr], axis=0)
                polar = dot(back_tab[...], spec)
                for s in range(2):
                    polar_buf[q, :, :, i + s, j * half:(j + 1) * half] = (
                        polar[:, s * half:(s + 1) * half].reshape(2, keep, half))
        parts_buf[q, mine, :, :, share] = polar_buf[q, :, pl.ds(me * kept, kept)]
        each(1, n, lambda d: out_copy(q, d).start())

    forward_stage(0)

    def step(q):
        @pl.when(q < stages - 1)
        def _():
            forward_stage(q + 1)
        compute_stage(q)

    each(0, stages, step)

    def reduce_stage(q):
        each(1, n, lambda d: out_copy(q, d).wait_recv())
        for part in range(2):
            total = parts_buf[q, 0, part]
            for other in range(1, groups):
                total = total + parts_buf[q, other, part]
            total_buf[q, part] = total
        for side in range(sides):
            near_if(side, False, lambda: near_copy(side, q).start())
        out_mine(q).start()

    each(0, stages, reduce_stage)

    def finish(q):
        out_mine(q).wait()
        for side in range(sides):
            near_if(side, False, lambda: near_copy(side, q).wait_send())
            near_if(side, True, lambda: near_copy(side, q).wait_recv())
        for k in range(2):
            each(1, group, lambda d: in_copy(k, q, d).wait_send())

            @pl.when(sends[k])
            def _():
                halo_copy(k, q).wait_send()
        each(1, n, lambda d: out_copy(q, d).wait_send())

    each(0, stages, finish)


def polarization(g_lesser, g_flipped, keep):
    n, rows = lax.axis_size("energy"), lax.axis_size("space")
    sides = 1 if rows == 2 else 2
    _, held, _, size, width = g_lesser.shape
    group = keep // held
    stages = size // group // ROWS
    less = g_lesser.reshape(2, held, group, stages, ROWS, width)
    great = g_flipped.reshape(2, held, group, stages, ROWS, width)
    tabs = tables(keep)
    any_spec = pl.BlockSpec(memory_space=pl.ANY)
    dma = pltpu.SemaphoreType.DMA
    block = pltpu.VMEM((stages, 2, keep, ROWS, width), jnp.float32)
    kept = keep // n
    shape = (2, kept, group, stages, ROWS, width)
    out, near = pl.pallas_call(
        functools.partial(correlate_kernel, n, group, rows),
        out_shape=[jax.ShapeDtypeStruct(s, jnp.float32) for s in (shape, (sides,) + shape)],
        in_specs=[pl.BlockSpec(memory_space=pltpu.VMEM)] * len(tabs) + [any_spec] * 2,
        out_specs=[any_spec] * 2,
        scratch_shapes=[
            block, block, block, block,
            pltpu.VMEM((stages, n // group, 2, kept, group, ROWS, width), jnp.float32),
            pltpu.VMEM((stages, 2, kept, group, ROWS, width), jnp.float32),
            dma((2, stages, group)), dma((2, stages, group)), dma((2, stages)),
            dma((2, stages)), dma((2, stages)),
            dma((stages, n)), dma((stages, n)), dma((stages,)),
            dma((sides, stages)), dma((sides, stages)),
        ],
        compiler_params=pltpu.CompilerParams(
            collective_id=0, has_side_effects=True, vmem_limit_bytes=56 * 2**20),
    )(*tabs, less, great)
    return out.reshape(2, kept, size, width), near.reshape(sides, 2, kept, size, width)


def shifted(block, axis, distance):
    devices = range(lax.axis_size(axis))
    return lax.ppermute(block, axis, [(i - distance, i) for i in devices if i - distance in devices])


def sandwich(left, middle, right):
    halfway = jnp.einsum("ab,cwbd->cwad", left, middle, precision=HIGH)
    return jnp.einsum("cwad,df->cwaf", halfway, right, precision=HIGH)


def local(g_lesser, g_greater, v_diag, v_upper):
    polar, near = polarization(g_lesser, jnp.swapaxes(g_greater, 3, 4), NW)
    rows = lax.axis_size("space")
    before = shifted(v_upper, "space", 1)[0]
    diag, upper = v_diag[0], v_upper[0]
    if rows == 2:
        coupling = jnp.where(lax.axis_index("space") == 0, upper, before.T)
        total = sandwich(diag, polar, diag) + sandwich(coupling, near[0], coupling.T)
    else:
        row = lax.axis_index("space")
        above = jnp.where(row > 0, near[0], 0.0)
        below = jnp.where(row < rows - 1, near[1], 0.0)
        total = sandwich(diag, polar, diag)
        total = total + sandwich(before.T, above, before) + sandwich(upper, below, upper.T)
    return total[:, :, None]


def solution(mesh):
    in_specs = (
        P(None, "energy", "space", None, None),
        P(None, "energy", "space", None, None),
        P("space", None, None),
        P("space", None, None),
    )
    out_specs = P(None, "energy", "space", None, None)
    return jax.shard_map(local, mesh=mesh, in_specs=in_specs, out_specs=out_specs, check_vma=False)
```

profile of v0, /device:TPU:21, one launch (start us, length us, event | category | flops | bytes accessed | tf_op | source)
XLA Modules:
  0.0 359.0 jit_solution(5265825415354363592)
XLA Ops:
  0.0 0.0 copy-start
  0.0 1.1 copy.14
  1.1 1.3 collective-permute-start
  2.4 8.7 %copy.13 = f32[2,16,1,256,256]{4,3,1,0,2:T(8,128)} copy(f32[2,16,1,256,256]{3,4,2,1,0:T(8,128)} %bitcast.54) | data formatting | bytes 16777216 | tf_op jit(solution)/shard_map/transpose | solution.py:279
  11.1 340.0 %shard_map.91 = (f32[2,4,4,8,8,256]{5,4,3,2,1,0:T(8,128)}, f32[1,2,4,4,8,8,256]{6,5,4,3,2,1,0:T(8,128)}) custom-call(bf16[256,768]{1,0:T(8,128)(2,1)} %constant.16.clone.less_wide, bf16[256,768]{1,0:T(8,128)(2,1)} %constant.17.clone.great_wide, bf16[256,384]{1,0:T(8,128)(2,1)} %constant.18.clone.less_narrow, bf16[256,384]{1,0:T(8,128)(2,1)} %constant.19.clone.great_narrow, ...), custom_call_target="tpu_custom_call" | custom-call | tf_op jit(solution)/shard_map/pallas_call | solution.py:248
  351.2 0.0 copy-done
  351.2 2.6 fusion.10
  353.8 0.0 copy-start.1
  353.8 0.0 copy-start.2
  353.8 1.0 fusion.2
  354.9 0.0 collective-permute-done
  354.9 0.0 copy-done.1
  354.9 0.6 copy-done.2
  355.5 1.1 fusion.7
  356.6 2.4 add_bitcast_fusion
Async XLA Ops:
  0.0 351.2 %copy-start = (f32[1,256,256]{2,1,0:T(8,128)S(1)}, f32[1,256,256]{2,1,0:T(8,128)}, u32[]{:S(2)}) copy-start(f32[1,256,256]{2,1,0:T(8,128)} %param.11) | copy-start | bytes 786436
  1.1 353.7 %collective-permute-start = (f32[1,256,256]{1,2,0:T(8,128)S(1)}, f32[1,256,256]{1,2,0:T(8,128)S(1)}, u32[]{:S(2)}, u32[]{:S(2)}) collective-permute-start(f32[1,256,256]{1,2,0:T(8,128)S(1)} %copy.14), channel_id=1, source_target_pairs={{0,1},{2,3},{4,5},{6,7},{8,9},{10,11},{12,13},{14,15},{16,17},{18,... | collective-permute-start | bytes 786440 | tf_op jit(solution)/shard_map/ppermute | solution.py:270
  353.8 1.1 copy-start.1
  353.8 1.7 copy-start.2
where the time goes:
time: 359 us
  Pallas kernels  340 us (95%)
  local copies, waits for them, and re-layouts  10.4 us (3%)
  matrix products  7.11 us (2%)
    pallas_call x1, Pallas kernels, polarization(): pl.pallas_call(functools.partial(correlate_kernel, n, group, rows), out_s...  340 us
    transpose x1, local copies, waits for them, and re-layouts, local(): polar, near = polarization(g_lesser, jnp.swapaxes(g_greater, 3, 4), NW)  8.7 us
  transfers between devices with their start and end apart: 1, of which 0 were waited for; matrix products, arithmetic and copies ran while one was open for 3% of the time, Pallas kernels for 95%

commit v1 on v0

v1 whole, which is shorter than its diff:
```python
import functools
import math

import jax
import jax.numpy as jnp
import numpy as np
from jax import lax
from jax.experimental import pallas as pl
from jax.experimental.pallas import tpu as pltpu
from jax.sharding import PartitionSpec as P

NW = 64
PREFACTOR = 0.0625
ROWS = 8
LANES = 128
AHEAD = 3
HIGH = lax.Precision.HIGH


def split_np(table):
    table = np.asarray(table, np.float64)
    high = table.astype(jnp.bfloat16)
    low = (table - high.astype(np.float64)).astype(jnp.bfloat16)
    return np.concatenate([high, low, high], axis=1)


def tables(keep):
    length = 2 * keep

    def forward(start, sign):
        phase = 2.0 * math.pi / length * (np.outer(np.arange(length), np.arange(start, start + keep)) % length)
        cos, sin = np.cos(phase), sign * np.sin(phase)
        return np.block([[cos, sin], [-sin, cos]])

    phase = 2.0 * math.pi / length * (np.outer(np.arange(keep), np.arange(length)) % length)
    cos, sin = np.cos(phase) * (PREFACTOR / length), np.sin(phase) * (PREFACTOR / length)
    back = np.block([[cos, -sin], [sin, cos]])
    wide = [np.concatenate([forward(0, sign), forward(keep, sign)], axis=1) for sign in (1, -1)]
    narrow = [forward(0, sign) for sign in (1, -1)]
    return [jnp.asarray(t) for t in (
        np.stack([split_np(t) for t in wide]), np.stack([split_np(t) for t in narrow]), split_np(back))]


def stacked(value):
    high = value.astype(jnp.bfloat16)
    low = (value - high.astype(jnp.float32)).astype(jnp.bfloat16)
    return jnp.concatenate([high, high, low], axis=0)


def dot(table, value):
    return jnp.dot(table, stacked(value), preferred_element_type=jnp.float32)


def correlate_kernel(
    n, group, rows, wide_tab, narrow_tab, back_tab, less, great, out, near,
    in_buf, halo_buf, polar_buf, chain_buf, final_buf,
    in_send, in_recv, own_sem, halo_send, halo_recv, chain_send, chain_recv,
    out_send, out_recv, out_own, near_send, near_recv,
):
    me = lax.axis_index("energy")
    mine, share = me // group, lax.rem(me, group)
    groups = n // group
    last = groups - 1
    sources = (less, great)
    held = less.shape[1]
    tiles = less.shape[3]
    row = lax.axis_index("space")
    sides = near.shape[0]
    stages = in_buf.shape[1]
    keep = in_buf.shape[3]
    kept = out.shape[1]
    block = group * kept
    mesh_id = pl.DeviceIdType.MESH

    def lanes_of(q):
        return pl.ds(pl.multiple_of(q // tiles * LANES, LANES), LANES)

    def in_copy(k, q, d):
        other = lax.rem(share + d, group)
        return pltpu.make_async_remote_copy(
            src_ref=sources[k].at[:, :, other, lax.rem(q, tiles), :, lanes_of(q)],
            dst_ref=in_buf.at[k, q, :, pl.ds(share * held, held)],
            send_sem=in_send.at[k, q, d],
            recv_sem=in_recv.at[k, q, d],
            device_id={"energy": mine * group + other},
            device_id_type=mesh_id,
        )

    def in_own(k, q):
        return pltpu.make_async_copy(
            sources[k].at[:, :, share, lax.rem(q, tiles), :, lanes_of(q)],
            in_buf.at[k, q, :, pl.ds(share * held, held)],
            own_sem.at[k, q],
        )

    def pivot(q):
        return lax.rem(q, groups)

    def halo_copy(k, q):
        peer = lax.rem(me + (group if k else n - group), n)
        return pltpu.make_async_remote_copy(
            src_ref=in_buf.at[k, q],
            dst_ref=halo_buf.at[q],
            send_sem=halo_send.at[k, q],
            recv_sem=halo_recv.at[q],
            device_id={"energy": peer},
            device_id_type=mesh_id,
        )

    def halo_sends(k, q):
        if k:
            return jnp.logical_and(mine >= pivot(q), mine < last)
        return jnp.logical_and(mine <= pivot(q), mine > 0)

    def chain_copy(up, q, j):
        peer = lax.rem(me + (group if up else n - group), n)
        return pltpu.make_async_remote_copy(
            src_ref=polar_buf.at[q, :, pl.ds(j * block, block)],
            dst_ref=chain_buf.at[q, j + up],
            send_sem=chain_send.at[up, q, j],
            recv_sem=chain_recv.at[up, q, j],
            device_id={"energy": peer},
            device_id_type=mesh_id,
        )

    def out_copy(q, d):
        other = lax.rem(share + d, group)
        return pltpu.make_async_remote_copy(
            src_ref=polar_buf.at[q, :, pl.ds((mine * group + other) * kept, kept)],
            dst_ref=final_buf.at[q, :, :, share],
            send_sem=out_send.at[q, d],
            recv_sem=out_recv.at[q, d],
            device_id={"energy": mine * group + other},
            device_id_type=mesh_id,
        )

    def out_mine(q):
        return pltpu.make_async_copy(
            final_buf.at[q], out.at[:, :, :, lax.rem(q, tiles), :, lanes_of(q)], out_own.at[q])

    def near_copy(side, q):
        return pltpu.make_async_remote_copy(
            src_ref=final_buf.at[q],
            dst_ref=near.at[side, :, :, :, lax.rem(q, tiles), :, lanes_of(q)],
            send_sem=near_send.at[side, q],
            recv_sem=near_recv.at[side, q],
            device_id={"space": lax.rem(row + (rows - 1 if side else 1), rows)},
            device_id_type=mesh_id,
        )

    def near_if(side, receiving, body):
        if rows == 2:
            body()
        else:
            pl.when(row > 0 if side != receiving else row < rows - 1)(body)

    def each(first, last, body):
        def step(d, carry):
            body(d)
            return carry
        lax.fori_loop(first, last, step, 0)

    barrier = pltpu.get_barrier_semaphore()
    each(1, n, lambda d: pl.semaphore_signal(
        barrier, inc=1, device_id={"energy": lax.rem(me + d, n)}, device_id_type=mesh_id))
    for side in range(sides):
        pl.semaphore_signal(
            barrier, inc=1, device_id={"space": lax.rem(row + (rows - 1 if side else 1), rows)}, device_id_type=mesh_id)
    pl.semaphore_wait(barrier, n - 1 + sides)

    def send_stage(q):
        for k in range(2):
            in_own(k, q).start()
            each(1, group, lambda d: in_copy(k, q, d).start())

    def forward_stage(q):
        for k in range(2):
            in_own(k, q).wait()
            each(1, group, lambda d: in_copy(k, q, d).wait_recv())

            @pl.when(halo_sends(k, q))
            def _():
                halo_copy(k, q).start()

    def pair(tile, i):
        return jnp.concatenate([tile[:, :, i + s].reshape(2 * keep, LANES) for s in range(2)], axis=1)

    def compute_stage(q):
        alone = mine == pivot(q)

        @pl.when(jnp.logical_not(alone))
        def _():
            halo_copy(0, q).wait_recv()

        @pl.when(alone)
        def _():
            halo_buf[q] = jnp.zeros(halo_buf.shape[1:], jnp.float32)

        wide = jnp.where(mine > pivot(q), 1, 0)
        for i in range(0, ROWS, 2):
            own = pair(in_buf.at[wide, q], i)
            other = pair(in_buf.at[1 - wide, q], i)
            halo = pair(halo_buf.at[q], i)
            spec_a = dot(wide_tab[wide], jnp.concatenate([own, halo], axis=0))
            spec_b = dot(narrow_tab[1 - wide], other)
            mid = spec_a.shape[0] // 2
            ar, ai, br, bi = spec_a[:mid], spec_a[mid:], spec_b[:mid], spec_b[mid:]
            spec = jnp.concatenate([ar * br - ai * bi, ar * bi + ai * br], axis=0)
            polar = dot(back_tab[...], spec)
            for s in range(2):
                polar_buf[q, :, :, i + s] = polar[:, s * LANES:(s + 1) * LANES].reshape(2, keep, LANES)

    def add_block(up, q, j):
        here = pl.ds(j * block, block)
        polar_buf[q, :, here] = polar_buf[q, :, here] + chain_buf[q, j + up]

    def chain_stage(up, q):
        far = 0 if up else last

        def hop(j):
            @pl.when(mine != far)
            def _():
                chain_copy(up, q, j).wait_recv()
                add_block(up, q, j)

            @pl.when(mine != j)
            def _():
                chain_copy(up, q, j).start()

        if up:
            each(0, last - mine + 1, lambda t: hop(last - t))
        else:
            each(0, mine + 1, hop)

    def final_stage(q):
        final_buf[q, :, :, share] = polar_buf[q, :, pl.ds(me * kept, kept)]
        each(1, group, lambda d: out_copy(q, d).start())

    def near_stage(q):
        each(1, group, lambda d: out_copy(q, d).wait_recv())
        for side in range(sides):
            near_if(side, False, lambda: near_copy(side, q).start())
        out_mine(q).start()

    def at(q, body):
        pl.when(jnp.logical_and(q >= 0, q < stages))(lambda: body(q))

    each(0, min(AHEAD, stages), send_stage)
    below = last - mine
    late = jnp.maximum(mine, below)

    def step(i):
        at(i + AHEAD, send_stage)
        at(i, forward_stage)
        at(i - 1, compute_stage)
        at(i - 1 - mine, lambda q: chain_stage(1, q))
        at(i - 1 - below, lambda q: chain_stage(0, q))
        at(i - 1 - late, final_stage)
        at(i - 2 - late - AHEAD, near_stage)

    each(0, stages + 2 + last + AHEAD, step)

    def finish(q):
        out_mine(q).wait()
        for side in range(sides):
            near_if(side, False, lambda: near_copy(side, q).wait_send())
            near_if(side, True, lambda: near_copy(side, q).wait_recv())
        for k in range(2):
            each(1, group, lambda d: in_copy(k, q, d).wait_send())

            @pl.when(halo_sends(k, q))
            def _():
                halo_copy(k, q).wait_send()
        each(mine + 1, groups, lambda j: chain_copy(1, q, j).wait_send())
        each(0, mine, lambda j: chain_copy(0, q, j).wait_send())
        each(1, group, lambda d: out_copy(q, d).wait_send())

    each(0, stages, finish)


def polarization(g_lesser, g_flipped, keep):
    n, rows = lax.axis_size("energy"), lax.axis_size("space")
    sides = 1 if rows == 2 else 2
    _, held, _, size, width = g_lesser.shape
    group = keep // held
    groups = n // group
    tiles = size // group // ROWS
    stages = tiles * (width // LANES)
    less = g_lesser.reshape(2, held, group, tiles, ROWS, width)
    great = g_flipped.reshape(2, held, group, tiles, ROWS, width)
    tabs = tables(keep)
    any_spec = pl.BlockSpec(memory_space=pl.ANY)
    dma = pltpu.SemaphoreType.DMA
    tile = (ROWS, LANES)
    kept = keep // n
    shape = (2, kept, group, tiles, ROWS, width)

    def vmem(*dims):
        return pltpu.VMEM(dims + tile, jnp.float32)

    out, near = pl.pallas_call(
        functools.partial(correlate_kernel, n, group, rows),
        out_shape=[jax.ShapeDtypeStruct(s, jnp.float32) for s in (shape, (sides,) + shape)],
        in_specs=[pl.BlockSpec(memory_space=pltpu.VMEM)] * len(tabs) + [any_spec] * 2,
        out_specs=[any_spec] * 2,
        scratch_shapes=[
            vmem(2, stages, 2, keep), vmem(stages, 2, keep), vmem(stages, 2, keep),
            vmem(stages, groups + 1, 2, group * kept), vmem(stages, 2, kept, group),
            dma((2, stages, group)), dma((2, stages, group)), dma((2, stages)),
            dma((2, stages)), dma((stages,)),
            dma((2, stages, groups)), dma((2, stages, groups)),
            dma((stages, group)), dma((stages, group)), dma((stages,)),
            dma((sides, stages)), dma((sides, stages)),
        ],
        compiler_params=pltpu.CompilerParams(
            collective_id=0, has_side_effects=True, vmem_limit_bytes=60 * 2**20),
    )(*tabs, less, great)
    return out.reshape(2, kept, size, width), near.reshape(sides, 2, kept, size, width)


def shifted(block, axis, distance):
    devices = range(lax.axis_size(axis))
    return lax.ppermute(block, axis, [(i - distance, i) for i in devices if i - distance in devices])


def sandwich(left, middle, right):
    halfway = jnp.einsum("ab,cwbd->cwad", left, middle, precision=HIGH)
    return jnp.einsum("cwad,df->cwaf", halfway, right, precision=HIGH)


def local(g_lesser, g_greater, v_diag, v_upper):
    polar, near = polarization(g_lesser, jnp.swapaxes(g_greater, 3, 4), NW)
    rows = lax.axis_size("space")
    before = shifted(v_upper, "space", 1)[0]
    diag, upper = v_diag[0], v_upper[0]
    if rows == 2:
        coupling = jnp.where(lax.axis_index("space") == 0, upper, before.T)
        total = sandwich(diag, polar, diag) + sandwich(coupling, near[0], coupling.T)
    else:
        row = lax.axis_index("space")
        above = jnp.where(row > 0, near[0], 0.0)
        below = jnp.where(row < rows - 1, near[1], 0.0)
        total = sandwich(diag, polar, diag)
        total = total + sandwich(before.T, above, before) + sandwich(upper, below, upper.T)
    return total[:, :, None]


def solution(mesh):
    in_specs = (
        P(None, "energy", "space", None, None),
        P(None, "energy", "space", None, None),
        P("space", None, None),
        P("space", None, None),
    )
    out_specs = P(None, "energy", "space", None, None)
    return jax.shard_map(local, mesh=mesh, in_specs=in_specs, out_specs=out_specs, check_vma=False)
```

time: 359 us -> 274 us (0.76)
  Pallas kernels: 340 us -> 252 us
    pallas_call x1, Pallas kernels: 340 us -> 252 us  [polarization(): pl.pallas_call(functools.partial(correlate_kernel, n, group, rows), out_s...]
  transfers between devices with their start and end apart: 1 -> 1, of which waited for: 0 -> 0; matrix products, arithmetic and copies ran while one was open for 3% -> 5% of each run, Pallas kernels for 95% -> 93%
where the time goes in v1:
time: 274 us; the launch traced here: 271 us
  Pallas kernels  252 us (92%)
  local copies, waits for them, and re-layouts  10.4 us (4%)
  matrix products  7.11 us (3%)
    pallas_call x1, Pallas kernels, polarization(): pl.pallas_call(functools.partial(correlate_kernel, n, group, rows), out_s...  252 us
    transpose x1, local copies, waits for them, and re-layouts, local(): polar, near = polarization(g_lesser, jnp.swapaxes(g_greater, 3, 4), NW)  8.7 us
  transfers between devices with their start and end apart: 1, of which 0 were waited for; matrix products, arithmetic and copies ran while one was open for 5% of the time, Pallas kernels for 93%

profile of v1, /device:TPU:21, one launch (start us, length us, event | category | flops | bytes accessed | tf_op | source)
XLA Modules:
  0.0 270.9 jit_solution(14846478687276479838)
XLA Ops:
  0.0 0.0 copy-start
  0.0 1.1 copy.12
  1.1 1.3 collective-permute-start
  2.4 8.7 %copy.11 = f32[2,16,1,256,256]{4,3,1,0,2:T(8,128)} copy(f32[2,16,1,256,256]{3,4,2,1,0:T(8,128)} %bitcast.54) | data formatting | bytes 16777216 | tf_op jit(solution)/shard_map/transpose | solution.py:332
  11.1 252.0 %shard_map.73 = (f32[2,4,4,8,8,256]{5,4,3,2,1,0:T(8,128)}, f32[1,2,4,4,8,8,256]{6,5,4,3,2,1,0:T(8,128)}) custom-call(bf16[2,256,768]{2,1,0:T(8,128)(2,1)} %constant.12.clone.wide_tab, bf16[2,256,384]{2,1,0:T(8,128)(2,1)} %constant.13.clone.narrow_tab, bf16[128,768]{1,0:T(8,128)(2,1)} %constant.14.clone.back_tab, f32[2,16,4,8,8,256]{5,4,3,2,1,0:T(8,128)} %bitcast.55, ...), custom_call_target="tpu_custom_call" | custom-call | tf_op jit(solution)/shard_map/pallas_call | solution.py:301
  263.1 0.0 copy-done
  263.1 2.6 fusion.10
  265.8 0.0 copy-start.1
  265.8 0.0 copy-start.2
  265.8 1.0 fusion.2
  266.8 0.0 collective-permute-done
  266.8 0.0 copy-done.1
  266.8 0.6 copy-done.2
  267.5 1.1 fusion.7
  268.5 2.4 add_bitcast_fusion
Async XLA Ops:
  0.0 263.1 %copy-start = (f32[1,256,256]{2,1,0:T(8,128)S(1)}, f32[1,256,256]{2,1,0:T(8,128)}, u32[]{:S(2)}) copy-start(f32[1,256,256]{2,1,0:T(8,128)} %param.9) | copy-start | bytes 786436
  1.1 265.7 %collective-permute-start = (f32[1,256,256]{1,2,0:T(8,128)S(1)}, f32[1,256,256]{1,2,0:T(8,128)S(1)}, u32[]{:S(2)}, u32[]{:S(2)}) collective-permute-start(f32[1,256,256]{1,2,0:T(8,128)S(1)} %copy.12), channel_id=1, source_target_pairs={{0,1},{2,3},{4,5},{6,7},{8,9},{10,11},{12,13},{14,15},{16,17},{18,... | collective-permute-start | bytes 786440 | tf_op jit(solution)/shard_map/ppermute | solution.py:323
  265.8 1.1 copy-start.1
  265.8 1.7 copy-start.2

commit v2 on v1

v2 whole, which is shorter than its diff:
```python
import functools
import math

import jax
import jax.numpy as jnp
import numpy as np
from jax import lax
from jax.experimental import pallas as pl
from jax.experimental.pallas import tpu as pltpu
from jax.sharding import PartitionSpec as P

NW = 64
PREFACTOR = 0.0625
ROWS = 8
LANES = 128
AHEAD = 2
PART = 64
SLOTS = 4


def split_np(table):
    table = np.asarray(table, np.float64)
    high = table.astype(jnp.bfloat16)
    low = (table - high.astype(np.float64)).astype(jnp.bfloat16)
    return np.concatenate([high, low, high], axis=1)


def tables(keep):
    length = 2 * keep

    def forward(start, sign):
        phase = 2.0 * math.pi / length * (np.outer(np.arange(length), np.arange(start, start + keep)) % length)
        cos, sin = np.cos(phase), sign * np.sin(phase)
        return np.block([[cos, sin], [-sin, cos]])

    phase = 2.0 * math.pi / length * (np.outer(np.arange(keep), np.arange(length)) % length)
    cos, sin = np.cos(phase) * (PREFACTOR / length), np.sin(phase) * (PREFACTOR / length)
    back = np.block([[cos, -sin], [sin, cos]])
    wide = [np.concatenate([forward(0, sign), forward(keep, sign)], axis=1) for sign in (1, -1)]
    narrow = [forward(0, sign) for sign in (1, -1)]
    return [jnp.asarray(t) for t in (
        np.stack([split_np(t) for t in wide]), np.stack([split_np(t) for t in narrow]), split_np(back))]


def split(value):
    high = value.astype(jnp.bfloat16)
    return high, (value - high.astype(jnp.float32)).astype(jnp.bfloat16)


def stacked(value):
    high, low = split(value)
    return jnp.concatenate([high, high, low], axis=0)


def spread(value):
    high, low = split(value)
    return jnp.concatenate([high, low, high], axis=1)


def product(left, right):
    return jnp.dot(left, right, preferred_element_type=jnp.float32)


def dot(table, value):
    return product(table, stacked(value))


def screening_kernel(
    n, group, rows, wide_tab, narrow_tab, back_tab, diag, upper, less, great, out,
    raw_buf, flip_buf, in_buf, halo_buf, chain_buf, final_buf, near_buf, half_buf, total_buf,
    before_buf, right_tab, left_tab,
    raw_sem, in_send, in_recv, own_sem, halo_send, halo_recv, chain_send, chain_recv,
    out_send, out_recv, near_send, near_recv, edge_sem, result_sem,
):
    me = lax.axis_index("energy")
    mine, share = me // group, lax.rem(me, group)
    groups = n // group
    last = groups - 1
    row = lax.axis_index("space")
    held, size, width = great.shape[1:]
    tiles = less.shape[2]
    sides = near_buf.shape[0]
    stages = in_buf.shape[1]
    keep = in_buf.shape[3]
    count = out.shape[0]
    kept = count // 2
    block = group * kept
    parts = left_tab.shape[0]
    per_part = tiles // parts
    mesh_id = pl.DeviceIdType.MESH

    def each(first, last, body):
        def step(d, carry):
            body(d)
            return carry
        lax.fori_loop(first, last, step, 0)

    def raw_copy(u):
        half, rest = u // (2 * held), lax.rem(u, 2 * held)
        slot = lax.rem(u, SLOTS)
        return pltpu.make_async_copy(
            great.at[rest // held, lax.rem(rest, held), pl.ds(pl.multiple_of(half * LANES, LANES), LANES)],
            raw_buf.at[slot], raw_sem.at[slot])

    def flip_half(half):
        first = half * 2 * held

        def flip(r):
            u = first + r
            raw_copy(u).wait()
            flip_buf[half, r // held, lax.rem(r, held)] = raw_buf[lax.rem(u, SLOTS)].T.reshape(
                tiles, group, ROWS, LANES)

            @pl.when(u + SLOTS < 2 * held * (width // LANES))
            def _():
                raw_copy(u + SLOTS).start()

        each(0, 2 * held, flip)

    def source(k, q, other):
        half, tile = q // tiles, lax.rem(q, tiles)
        if k:
            return flip_buf.at[half, :, :, tile, other]
        return less.at[:, :, tile, other, :, pl.ds(pl.multiple_of(half * LANES, LANES), LANES)]

    def in_copy(k, q, d):
        other = lax.rem(share + d, group)
        return pltpu.make_async_remote_copy(
            src_ref=source(k, q, other),
            dst_ref=in_buf.at[k, q, :, pl.ds(share * held, held)],
            send_sem=in_send.at[k, q, d],
            recv_sem=in_recv.at[k, q, d],
            device_id={"energy": mine * group + other},
            device_id_type=mesh_id,
        )

    def in_own(k, q):
        return pltpu.make_async_copy(
            source(k, q, share), in_buf.at[k, q, :, pl.ds(share * held, held)], own_sem.at[k, q])

    def pivot(q):
        return lax.rem(q, groups)

    def halo_copy(k, q):
        peer = lax.rem(me + (group if k else n - group), n)
        return pltpu.make_async_remote_copy(
            src_ref=in_buf.at[k, q],
            dst_ref=halo_buf.at[q],
            send_sem=halo_send.at[k, q],
            recv_sem=halo_recv.at[q],
            device_id={"energy": peer},
            device_id_type=mesh_id,
        )

    def halo_sends(k, q):
        if k:
            return jnp.logical_and(mine >= pivot(q), mine < last)
        return jnp.logical_and(mine <= pivot(q), mine > 0)

    def polar_slot(q):
        return jnp.where(jnp.logical_or(mine < pivot(q), mine == last), 1, 0)

    def slot_sent(q):
        return jnp.logical_and(mine == pivot(q), jnp.logical_and(mine > 0, mine < last))

    def chain_copy(up, q, j):
        peer = lax.rem(me + (group if up else n - group), n)
        return pltpu.make_async_remote_copy(
            src_ref=in_buf.at[polar_slot(q), q, :, pl.ds(j * block, block)],
            dst_ref=chain_buf.at[q, j + up],
            send_sem=chain_send.at[up, q, j],
            recv_sem=chain_recv.at[up, q, j],
            device_id={"energy": peer},
            device_id_type=mesh_id,
        )

    def out_copy(q, d):
        other = lax.rem(share + d, group)
        return pltpu.make_async_remote_copy(
            src_ref=in_buf.at[polar_slot(q), q, :, pl.ds((mine * group + other) * kept, kept)],
            dst_ref=final_buf.at[q, :, :, share],
            send_sem=out_send.at[q, d],
            recv_sem=out_recv.at[q, d],
            device_id={"energy": mine * group + other},
            device_id_type=mesh_id,
        )

    def near_copy(side, q):
        return pltpu.make_async_remote_copy(
            src_ref=final_buf.at[q],
            dst_ref=near_buf.at[side, q],
            send_sem=near_send.at[side, q],
            recv_sem=near_recv.at[side, q],
            device_id={"space": lax.rem(row + (rows - 1 if side else 1), rows)},
            device_id_type=mesh_id,
        )

    def near_if(side, receiving, body, other=None):
        if rows == 2:
            body()
        else:
            there = row > 0 if bool(side) != receiving else row < rows - 1
            pl.when(there)(body)
            if other is not None:
                pl.when(jnp.logical_not(there))(other)

    def edge_copy():
        return pltpu.make_async_remote_copy(
            src_ref=upper,
            dst_ref=before_buf,
            send_sem=edge_sem.at[0],
            recv_sem=edge_sem.at[1],
            device_id={"space": lax.rem(row + 1, rows)},
            device_id_type=mesh_id,
        )

    def result_copy(item):
        return pltpu.make_async_copy(total_buf.at[item], out.at[item], result_sem.at[item])

    each(0, SLOTS, lambda u: raw_copy(u).start())
    barrier = pltpu.get_barrier_semaphore()
    each(1, n, lambda d: pl.semaphore_signal(
        barrier, inc=1, device_id={"energy": lax.rem(me + d, n)}, device_id_type=mesh_id))
    for side in range(sides):
        pl.semaphore_signal(
            barrier, inc=1, device_id={"space": lax.rem(row + (rows - 1 if side else 1), rows)}, device_id_type=mesh_id)
    pl.semaphore_wait(barrier, n - 1 + sides)

    def send_kind(k, q):
        in_own(k, q).start()
        each(1, group, lambda d: in_copy(k, q, d).start())

    def send_stage(q):
        for k in range(2):
            send_kind(k, q)

    def prepare():
        edge_copy().wait()
        before, above = before_buf[...], upper[...]
        if rows == 2:
            link = jnp.where(row == 0, above, before)
            turned = link.T
            couplings = [(jnp.where(row == 0, link, turned), jnp.where(row == 0, turned, link))]
        else:
            before = jnp.where(row > 0, before, 0.0)
            above = jnp.where(row < rows - 1, above, 0.0)
            couplings = [(before.T, before), (above, above.T)]
        pairs = [(diag[...], diag[...])] + couplings
        for side, (_, right) in enumerate(pairs):
            for half in range(width // LANES):
                right_tab[side, half] = stacked(right[half * LANES:(half + 1) * LANES])
        for part in range(parts):
            columns = slice(part * PART, (part + 1) * PART)
            left_tab[part] = jnp.concatenate([spread(left[:, columns]) for left, _ in pairs], axis=1)

    def forward_stage(q):
        for k in range(2):
            in_own(k, q).wait()
            each(1, group, lambda d: in_copy(k, q, d).wait_recv())

            @pl.when(halo_sends(k, q))
            def _():
                halo_copy(k, q).start()

    def pair(tile, i):
        return jnp.concatenate([tile[:, :, i + s].reshape(2 * keep, LANES) for s in range(2)], axis=1)

    def compute_stage(q):
        alone = mine == pivot(q)

        @pl.when(jnp.logical_not(alone))
        def _():
            halo_copy(0, q).wait_recv()

        @pl.when(alone)
        def _():
            halo_buf[q] = jnp.zeros(halo_buf.shape[1:], jnp.float32)

        @pl.when(slot_sent(q))
        def _():
            halo_copy(0, q).wait_send()

        wide = jnp.where(mine > pivot(q), 1, 0)
        slot = polar_slot(q)
        for i in range(0, ROWS, 2):
            own = pair(in_buf.at[wide, q], i)
            other = pair(in_buf.at[1 - wide, q], i)
            halo = pair(halo_buf.at[q], i)
            spec_a = dot(wide_tab[wide], jnp.concatenate([own, halo], axis=0))
            spec_b = dot(narrow_tab[1 - wide], other)
            mid = spec_a.shape[0] // 2
            ar, ai, br, bi = spec_a[:mid], spec_a[mid:], spec_b[:mid], spec_b[mid:]
            spec = jnp.concatenate([ar * br - ai * bi, ar * bi + ai * br], axis=0)
            polar = dot(back_tab[...], spec)
            for s in range(2):
                in_buf[slot, q, :, :, i + s] = polar[:, s * LANES:(s + 1) * LANES].reshape(2, keep, LANES)

    def chain_stage(up, q):
        far = 0 if up else last
        slot = polar_slot(q)

        def hop(j):
            @pl.when(mine != far)
            def _():
                chain_copy(up, q, j).wait_recv()
                here = pl.ds(j * block, block)
                in_buf[slot, q, :, here] = in_buf[slot, q, :, here] + chain_buf[q, j + up]

            @pl.when(mine != j)
            def _():
                chain_copy(up, q, j).start()

        if up:
            each(0, last - mine + 1, lambda t: hop(last - t))
        else:
            each(0, mine + 1, hop)

    def final_stage(q):
        final_buf[q, :, :, share] = in_buf[polar_slot(q), q, :, pl.ds(me * kept, kept)]
        each(1, group, lambda d: out_copy(q, d).start())

    def halfway(side, q, value):
        half, tile = q // tiles, lax.rem(q, tiles)
        term = product(spread(value.reshape(count * group * ROWS, LANES)), right_tab[side, half])
        half_buf[side, :, tile] = half_buf[side, :, tile] + term.reshape(count, group, ROWS, width)

    def near_stage(q):
        each(1, group, lambda d: out_copy(q, d).wait_recv())
        for side in range(sides):
            near_if(side, False, lambda: near_copy(side, q).start())
        halfway(0, q, final_buf[q])

    def screen_part(part):
        def one(item):
            terms = [
                stacked(half_buf[side, item, pl.ds(part * per_part, per_part)].reshape(PART, width))
                for side in range(1 + sides)
            ]
            total_buf[item] = total_buf[item] + product(left_tab[part], jnp.concatenate(terms, axis=0))

            @pl.when(part == parts - 1)
            def _():
                result_copy(item).start()

        each(0, count, one)

    def screen_stage(q):
        for side in range(sides):
            def arrived():
                near_copy(side, q).wait_recv()
                halfway(1 + side, q, near_buf[side, q])
            near_if(side, True, arrived)
        done = q + 1 - (stages - tiles)

        @pl.when(jnp.logical_and(done > 0, lax.rem(done, per_part) == 0))
        def _():
            screen_part(done // per_part - 1)

    def at(q, body):
        pl.when(jnp.logical_and(q >= 0, q < stages))(lambda: body(q))

    edge_copy().start()
    ahead = min(AHEAD, tiles)
    each(0, ahead, lambda q: send_kind(0, q))
    flip_half(0)
    each(0, ahead, lambda q: send_kind(1, q))
    for half in range(1, width // LANES):
        flip_half(half)
    half_buf[...] = jnp.zeros(half_buf.shape, jnp.float32)
    total_buf[...] = jnp.zeros(total_buf.shape, jnp.float32)
    prepare()
    below = last - mine
    late = jnp.maximum(mine, below)

    def step(i):
        at(i + ahead, send_stage)
        at(i, forward_stage)
        at(i - 1, compute_stage)
        at(i - 1 - mine, lambda q: chain_stage(1, q))
        at(i - 1 - below, lambda q: chain_stage(0, q))
        at(i - 1 - late, final_stage)
        at(i - 2 - late - ahead, near_stage)
        at(i - 3 - late - ahead, screen_stage)

    each(0, stages + 3 + last + ahead, step)

    def finish(q):
        for side in range(sides):
            near_if(side, False, lambda: near_copy(side, q).wait_send())
        for k in range(2):
            each(1, group, lambda d: in_copy(k, q, d).wait_send())

            @pl.when(jnp.logical_and(halo_sends(k, q), jnp.logical_not(slot_sent(q))) if k == 0 else halo_sends(k, q))
            def _():
                halo_copy(k, q).wait_send()
        each(mine + 1, groups, lambda j: chain_copy(1, q, j).wait_send())
        each(0, mine, lambda j: chain_copy(0, q, j).wait_send())
        each(1, group, lambda d: out_copy(q, d).wait_send())

    each(0, stages, finish)
    each(0, count, lambda item: result_copy(item).wait())


def local(g_lesser, g_greater, v_diag, v_upper):
    n, rows = lax.axis_size("energy"), lax.axis_size("space")
    sides = 1 if rows == 2 else 2
    _, held, _, size, width = g_lesser.shape
    keep = NW
    group = keep // held
    groups = n // group
    tiles = size // group // ROWS
    halves = width // LANES
    stages = tiles * halves
    kept = keep // n
    parts = size // PART
    less = g_lesser.reshape(2, held, tiles, group, ROWS, width)
    great = g_greater.reshape(2, held, size, width)
    tabs = tables(keep)
    vmem_spec = pl.BlockSpec(memory_space=pltpu.VMEM)
    any_spec = pl.BlockSpec(memory_space=pl.ANY)
    dma = pltpu.SemaphoreType.DMA

    def vmem(*dims, dtype=jnp.float32):
        return pltpu.VMEM(dims, dtype)

    def tiled(*dims):
        return vmem(*dims, ROWS, LANES)

    out = pl.pallas_call(
        functools.partial(screening_kernel, n, group, rows),
        out_shape=jax.ShapeDtypeStruct((2 * kept, size, width), jnp.float32),
        in_specs=[vmem_spec] * (len(tabs) + 2) + [any_spec] * 2,
        out_specs=any_spec,
        scratch_shapes=[
            vmem(SLOTS, LANES, width),
            tiled(halves, 2, held, tiles, group),
            tiled(2, stages, 2, keep),
            tiled(stages, 2, keep),
            tiled(stages, groups + 1, 2, group * kept),
            tiled(stages, 2, kept, group),
            tiled(sides, stages, 2, kept, group),
            vmem(1 + sides, 2 * kept, tiles, group, ROWS, width),
            vmem(2 * kept, size, width),
            vmem(size, width),
            vmem(1 + sides, halves, 3 * LANES, width, dtype=jnp.bfloat16),
            vmem(parts, size, 3 * PART * (1 + sides), dtype=jnp.bfloat16),
            dma((SLOTS,)),
            dma((2, stages, group)), dma((2, stages, group)), dma((2, stages)),
            dma((2, stages)), dma((stages,)),
            dma((2, stages, groups)), dma((2, stages, groups)),
            dma((stages, group)), dma((stages, group)),
            dma((sides, stages)), dma((sides, stages)),
            dma((2,)), dma((2 * kept,)),
        ],
        compiler_params=pltpu.CompilerParams(
            collective_id=0, has_side_effects=True, vmem_limit_bytes=2**26 - 2**16),
    )(*tabs, v_diag[0], v_upper[0], less, great)
    return out.reshape(2, kept, 1, size, width)


def solution(mesh):
    in_specs = (
        P(None, "energy", "space", None, None),
        P(None, "energy", "space", None, None),
        P("space", None, None),
        P("space", None, None),
    )
    out_specs = P(None, "energy", "space", None, None)
    return jax.shard_map(local, mesh=mesh, in_specs=in_specs, out_specs=out_specs, check_vma=False)
```

time: 274 us -> 261 us (0.953)
  local copies, waits for them, and re-layouts: 10.4 us -> 3.05 us
  matrix products: 7.11 us -> 0 us
    transpose x1 -> x0, local copies, waits for them, and re-layouts: 8.7 us -> none  [local(): polar, near = polarization(g_lesser, jnp.swapaxes(g_greater, 3, 4), NW)]
    dot_general x4 -> x0, matrix products: 7.11 us -> none  [the longest x2 3.7 us: sandwich(): halfway = jnp.einsum('ab,cwbd->cwad', left, middle, precision=HIGH)]
  transfers between devices with their start and end apart: 1 -> 0, of which waited for: 0 -> 0; matrix products, arithmetic and copies ran while one was open for 5% -> 0% of each run, Pallas kernels for 93% -> 0%
where the time goes in v2:
time: 261 us; the launch traced here: 257 us
  Pallas kernels  254 us (97%)
  local copies, waits for them, and re-layouts  3.05 us (1%)
    pallas_call x1, Pallas kernels, local(): pl.pallas_call(functools.partial(screening_kernel, n, group, rows), out_s...  254 us

profile of v2, /device:TPU:21, one launch (start us, length us, event | category | flops | bytes accessed | tf_op | source)
XLA Modules:
  0.0 257.2 jit_solution(7771360159139945211)
XLA Ops:
  0.0 254.2 %shard_map.73 = f32[8,256,256]{2,1,0:T(8,128)} custom-call(bf16[2,256,768]{2,1,0:T(8,128)(2,1)} %constant.6.clone.wide_tab, bf16[2,256,384]{2,1,0:T(8,128)(2,1)} %constant.7.clone.narrow_tab, bf16[128,768]{1,0:T(8,128)(2,1)} %constant.8.clone.back_tab, f32[256,256]{1,0:T(8,128)} %bitcast.10, f32[256,256]{1,0:T(8,128)} %bitcast.11, ...), custom_call_target="tpu_custom_call" | custom-call | tf_op jit(solution)/shard_map/pallas_call | solution.py:429
  254.2 3.0 %copy.10 = f32[2,4,1,256,256]{4,3,2,1,0:T(8,128)} copy(f32[2,4,1,256,256]{4,3,2,1,0:T(8,128)} %bitcast.7) | data formatting | bytes 4194304

commit v3 on v2

--- a/solution.py
+++ b/solution.py
@@ -13,7 +13,15 @@
 PREFACTOR = 0.0625
 ROWS = 8
 LANES = 128
-AHEAD = 2
+AHEAD = 3
+FIRST = 4
+EARLY = 12
+READY = 3
+HOP = 4
+TURN = 4
+NEAR = 3
+SCREEN = 4
+CORES = 2
 PART = 64
 SLOTS = 4
 
@@ -69,8 +77,8 @@
     n, group, rows, wide_tab, narrow_tab, back_tab, diag, upper, less, great, out,
     raw_buf, flip_buf, in_buf, halo_buf, chain_buf, final_buf, near_buf, half_buf, total_buf,
     before_buf, right_tab, left_tab,
-    raw_sem, in_send, in_recv, own_sem, halo_send, halo_recv, chain_send, chain_recv,
-    out_send, out_recv, near_send, near_recv, edge_sem, result_sem,
+    raw_sem, in_send, in_recv, own_sem, mate_send, mate_recv, halo_send, halo_recv, chain_send, chain_recv,
+    out_send, out_recv, close_send, close_recv, near_send, near_recv, edge_sem, result_sem,
 ):
     me = lax.axis_index("energy")
     mine, share = me // group, lax.rem(me, group)
@@ -87,6 +95,8 @@
     block = group * kept
     parts = left_tab.shape[0]
     per_part = tiles // parts
+    cores = mate_recv.shape[1]
+    chip, core, chips = share // cores, lax.rem(share, cores), group // cores
     mesh_id = pl.DeviceIdType.MESH
 
     def each(first, last, body):
@@ -139,16 +149,41 @@
             source(k, q, share), in_buf.at[k, q, :, pl.ds(share * held, held)], own_sem.at[k, q])
 
     def pivot(q):
-        return lax.rem(q, groups)
-
-    def halo_copy(k, q):
-        peer = lax.rem(me + (group if k else n - group), n)
-        return pltpu.make_async_remote_copy(
-            src_ref=in_buf.at[k, q],
-            dst_ref=halo_buf.at[q],
-            send_sem=halo_send.at[k, q],
-            recv_sem=halo_recv.at[q],
-            device_id={"energy": peer},
+        outer = q * ((groups + 1) // 2) // stages
+        return jnp.where(lax.rem(q, 2) == 0, outer, last - outer)
+
+    def beside(k):
+        return lax.rem(mine + (1 if k else groups - 1), groups)
+
+    def mate_copy(k, q, c):
+        there = chip * cores + c
+        return pltpu.make_async_remote_copy(
+            src_ref=source(k, q, there),
+            dst_ref=halo_buf.at[q, :, pl.ds(share * held, held)],
+            send_sem=mate_send.at[k, q, c],
+            recv_sem=mate_recv.at[q, core],
+            device_id={"energy": beside(k) * group + there},
+            device_id_type=mesh_id,
+        )
+
+    def mate_wait(q, c):
+        pltpu.make_async_remote_copy(
+            src_ref=source(0, q, share),
+            dst_ref=halo_buf.at[q, :, pl.ds((chip * cores + c) * held, held)],
+            send_sem=mate_send.at[0, q, c],
+            recv_sem=mate_recv.at[q, c],
+            device_id={"energy": beside(0) * group + share},
+            device_id_type=mesh_id,
+        ).wait_recv()
+
+    def halo_copy(k, q, d):
+        energies = pl.ds(lax.rem(chip + d, chips) * cores * held, cores * held)
+        return pltpu.make_async_remote_copy(
+            src_ref=in_buf.at[k, q, :, energies],
+            dst_ref=halo_buf.at[q, :, energies],
+            send_sem=halo_send.at[k, q, d],
+            recv_sem=halo_recv.at[q, d],
+            device_id={"energy": beside(k) * group + share},
             device_id_type=mesh_id,
         )
 
@@ -185,13 +220,38 @@
             device_id_type=mesh_id,
         )
 
-    def near_copy(side, q):
-        return pltpu.make_async_remote_copy(
-            src_ref=final_buf.at[q],
-            dst_ref=near_buf.at[side, q],
-            send_sem=near_send.at[side, q],
-            recv_sem=near_recv.at[side, q],
-            device_id={"space": lax.rem(row + (rows - 1 if side else 1), rows)},
+    def row_of(side):
+        return lax.rem(row + (rows - 1 if side else 1), rows)
+
+    def close_copy(side, q, c):
+        there = mine * group + chip * cores + c
+        return pltpu.make_async_remote_copy(
+            src_ref=in_buf.at[polar_slot(q), q, :, pl.ds(there * kept, kept)],
+            dst_ref=near_buf.at[side, q, :, :, share],
+            send_sem=close_send.at[side, q, c],
+            recv_sem=close_recv.at[side, q, core],
+            device_id={"energy": there, "space": row_of(side)},
+            device_id_type=mesh_id,
+        )
+
+    def close_wait(side, q, c):
+        pltpu.make_async_remote_copy(
+            src_ref=in_buf.at[0, q, :, pl.ds(0, kept)],
+            dst_ref=near_buf.at[side, q, :, :, chip * cores + c],
+            send_sem=close_send.at[side, q, c],
+            recv_sem=close_recv.at[side, q, c],
+            device_id={"space": row_of(side)},
+            device_id_type=mesh_id,
+        ).wait_recv()
+
+    def near_copy(side, q, d):
+        shares = pl.ds(lax.rem(chip + d, chips) * cores, cores)
+        return pltpu.make_async_remote_copy(
+            src_ref=final_buf.at[q, :, :, shares],
+            dst_ref=near_buf.at[side, q, :, :, shares],
+            send_sem=near_send.at[side, q, d],
+            recv_sem=near_recv.at[side, q, d],
+            device_id={"space": row_of(side)},
             device_id_type=mesh_id,
         )
 
@@ -222,17 +282,19 @@
     each(1, n, lambda d: pl.semaphore_signal(
         barrier, inc=1, device_id={"energy": lax.rem(me + d, n)}, device_id_type=mesh_id))
     for side in range(sides):
-        pl.semaphore_signal(
-            barrier, inc=1, device_id={"space": lax.rem(row + (rows - 1 if side else 1), rows)}, device_id_type=mesh_id)
-    pl.semaphore_wait(barrier, n - 1 + sides)
+        each(0, cores, lambda c: pl.semaphore_signal(
+            barrier, inc=1, device_id={"energy": mine * group + chip * cores + c, "space": row_of(side)},
+            device_id_type=mesh_id))
+    pl.semaphore_wait(barrier, n - 1 + sides * cores)
 
     def send_kind(k, q):
         in_own(k, q).start()
         each(1, group, lambda d: in_copy(k, q, d).start())
 
-    def send_stage(q):
-        for k in range(2):
-            send_kind(k, q)
+    def mate_kind(k, q):
+        @pl.when(halo_sends(k, q))
+        def _():
+            each(0, cores, lambda c: mate_copy(k, q, c).start())
 
     def prepare():
         edge_copy().wait()
@@ -253,14 +315,13 @@
             columns = slice(part * PART, (part + 1) * PART)
             left_tab[part] = jnp.concatenate([spread(left[:, columns]) for left, _ in pairs], axis=1)
 
-    def forward_stage(q):
-        for k in range(2):
-            in_own(k, q).wait()
-            each(1, group, lambda d: in_copy(k, q, d).wait_recv())
-
-            @pl.when(halo_sends(k, q))
-            def _():
-                halo_copy(k, q).start()
+    def forward_kind(k, q):
+        in_own(k, q).wait()
+        each(1, group, lambda d: in_copy(k, q, d).wait_recv())
+
+        @pl.when(halo_sends(k, q))
+        def _():
+            each(1, chips, lambda d: halo_copy(k, q, d).start())
 
     def pair(tile, i):
         return jnp.concatenate([tile[:, :, i + s].reshape(2 * keep, LANES) for s in range(2)], axis=1)
@@ -270,7 +331,8 @@
 
         @pl.when(jnp.logical_not(alone))
         def _():
-            halo_copy(0, q).wait_recv()
+            each(0, cores, lambda c: mate_wait(q, c))
+            each(1, chips, lambda d: halo_copy(0, q, d).wait_recv())
 
         @pl.when(alone)
         def _():
@@ -278,7 +340,7 @@
 
         @pl.when(slot_sent(q))
         def _():
-            halo_copy(0, q).wait_send()
+            each(1, chips, lambda d: halo_copy(0, q, d).wait_send())
 
         wide = jnp.where(mine > pivot(q), 1, 0)
         slot = polar_slot(q)
@@ -317,6 +379,10 @@
 
     def final_stage(q):
         final_buf[q, :, :, share] = in_buf[polar_slot(q), q, :, pl.ds(me * kept, kept)]
+        for side in range(sides):
+            near_if(side, False, lambda: each(0, cores, lambda c: close_copy(side, q, c).start()))
+
+    def out_stage(q):
         each(1, group, lambda d: out_copy(q, d).start())
 
     def halfway(side, q, value):
@@ -327,7 +393,7 @@
     def near_stage(q):
         each(1, group, lambda d: out_copy(q, d).wait_recv())
         for side in range(sides):
-            near_if(side, False, lambda: near_copy(side, q).start())
+            near_if(side, False, lambda: each(1, chips, lambda d: near_copy(side, q, d).start()))
         halfway(0, q, final_buf[q])
 
     def screen_part(part):
@@ -347,7 +413,8 @@
     def screen_stage(q):
         for side in range(sides):
             def arrived():
-                near_copy(side, q).wait_recv()
+                each(0, cores, lambda c: close_wait(side, q, c))
+                each(1, chips, lambda d: near_copy(side, q, d).wait_recv())
                 halfway(1 + side, q, near_buf[side, q])
             near_if(side, True, arrived)
         done = q + 1 - (stages - tiles)
@@ -356,43 +423,70 @@
         def _():
             screen_part(done // per_part - 1)
 
-    def at(q, body):
-        pl.when(jnp.logical_and(q >= 0, q < stages))(lambda: body(q))
-
+    def by_kind(v, begin, body):
+        for k in range(2):
+            @pl.when(jnp.logical_and(lax.rem(v, 2) == k, jnp.logical_and(v >= begin, v < 2 * stages)))
+            def _():
+                body(k, v // 2)
+
+    def at(v, body):
+        ready = jnp.logical_and(v >= 0, v < 2 * stages)
+        pl.when(jnp.logical_and(ready, lax.rem(v, 2) == 0))(lambda: body(v // 2))
+
+    def clear():
+        half_buf[...] = jnp.zeros(half_buf.shape, jnp.float32)
+        total_buf[...] = jnp.zeros(total_buf.shape, jnp.float32)
+
+    first, early = min(FIRST, 2 * tiles), min(EARLY, 2 * tiles)
+    send_kind(0, 0)
+    each(0, early // 2, lambda q: mate_kind(0, q))
     edge_copy().start()
-    ahead = min(AHEAD, tiles)
-    each(0, ahead, lambda q: send_kind(0, q))
     flip_half(0)
-    each(0, ahead, lambda q: send_kind(1, q))
-    for half in range(1, width // LANES):
-        flip_half(half)
-    half_buf[...] = jnp.zeros(half_buf.shape, jnp.float32)
-    total_buf[...] = jnp.zeros(total_buf.shape, jnp.float32)
-    prepare()
+    each(1, first, lambda v: by_kind(v, 1, send_kind))
+    each(0, early // 2, lambda q: mate_kind(1, q))
+    clear()
     below = last - mine
-    late = jnp.maximum(mine, below)
-
-    def step(i):
-        at(i + ahead, send_stage)
-        at(i, forward_stage)
-        at(i - 1, compute_stage)
-        at(i - 1 - mine, lambda q: chain_stage(1, q))
-        at(i - 1 - below, lambda q: chain_stage(0, q))
-        at(i - 1 - late, final_stage)
-        at(i - 2 - late - ahead, near_stage)
-        at(i - 3 - late - ahead, screen_stage)
-
-    each(0, stages + 3 + last + ahead, step)
+    settled = READY + HOP * jnp.maximum(mine, below)
+    turn = max(2 * stages - TURN, 0)
+
+    def turned(v, body):
+        steady = v >= 2 * turn - settled
+        q = jnp.where(steady, (v - settled) // 2, v - turn)
+        begun = jnp.where(steady, jnp.where(v >= settled, lax.rem(v - settled, 2) == 0, False), v >= turn)
+        pl.when(jnp.logical_and(begun, q < stages))(lambda: body(q))
+
+    def step(u):
+        by_kind(u + AHEAD, first, send_kind)
+        by_kind(u + early, early, mate_kind)
+        by_kind(u, 0, forward_kind)
+        for half in range(1, width // LANES):
+            pl.when(u == 0)(lambda: flip_half(half))
+        pl.when(u == 1)(prepare)
+        at(u - READY, compute_stage)
+        at(u - READY - HOP * mine, lambda q: chain_stage(1, q))
+        at(u - READY - HOP * below, lambda q: chain_stage(0, q))
+        at(u - settled, final_stage)
+        turned(u, out_stage)
+        turned(u - NEAR, near_stage)
+        turned(u - NEAR - SCREEN, screen_stage)
+
+    length = max(2 * stages - 1 + READY + HOP * last, turn + stages)
+    each(0, length + NEAR + SCREEN, step)
 
     def finish(q):
         for side in range(sides):
-            near_if(side, False, lambda: near_copy(side, q).wait_send())
+            near_if(side, False, lambda: each(0, cores, lambda c: close_copy(side, q, c).wait_send()))
+            near_if(side, False, lambda: each(1, chips, lambda d: near_copy(side, q, d).wait_send()))
         for k in range(2):
             each(1, group, lambda d: in_copy(k, q, d).wait_send())
 
             @pl.when(jnp.logical_and(halo_sends(k, q), jnp.logical_not(slot_sent(q))) if k == 0 else halo_sends(k, q))
             def _():
-                halo_copy(k, q).wait_send()
+                each(1, chips, lambda d: halo_copy(k, q, d).wait_send())
+
+            @pl.when(halo_sends(k, q))
+            def _():
+                each(0, cores, lambda c: mate_copy(k, q, c).wait_send())
         each(mine + 1, groups, lambda j: chain_copy(1, q, j).wait_send())
         each(0, mine, lambda j: chain_copy(0, q, j).wait_send())
         each(1, group, lambda d: out_copy(q, d).wait_send())
@@ -413,6 +507,7 @@
     stages = tiles * halves
     kept = keep // n
     parts = size // PART
+    cores = CORES if group % CORES == 0 else 1
     less = g_lesser.reshape(2, held, tiles, group, ROWS, width)
     great = g_greater.reshape(2, held, size, width)
     tabs = tables(keep)
@@ -446,10 +541,12 @@
             vmem(parts, size, 3 * PART * (1 + sides), dtype=jnp.bfloat16),
             dma((SLOTS,)),
             dma((2, stages, group)), dma((2, stages, group)), dma((2, stages)),
-            dma((2, stages)), dma((stages,)),
+            dma((2, stages, cores)), dma((stages, cores)),
+            dma((2, stages, group // cores)), dma((stages, group // cores)),
             dma((2, stages, groups)), dma((2, stages, groups)),
             dma((stages, group)), dma((stages, group)),
-            dma((sides, stages)), dma((sides, stages)),
+            dma((sides, stages, cores)), dma((sides, stages, cores)),
+            dma((sides, stages, group // cores)), dma((sides, stages, group // cores)),
             dma((2,)), dma((2 * kept,)),
         ],
         compiler_params=pltpu.CompilerParams(

time: 261 us -> 247 us (0.946)
  Pallas kernels: 254 us -> 241 us
    pallas_call x1, Pallas kernels: 254 us -> 241 us  [local(): pl.pallas_call(functools.partial(screening_kernel, n, group, rows), out_s...]
where the time goes in v3:
time: 247 us; the launch traced here: 244 us
  Pallas kernels  241 us (98%)
  local copies, waits for them, and re-layouts  3.05 us (1%)
    pallas_call x1, Pallas kernels, local(): pl.pallas_call(functools.partial(screening_kernel, n, group, rows), out_s...  241 us

profile of v3, /device:TPU:21, one launch (start us, length us, event | category | flops | bytes accessed | tf_op | source)
XLA Modules:
  0.0 244.3 jit_solution(11864328132985385462)
XLA Ops:
  0.0 241.3 %shard_map.73 = f32[8,256,256]{2,1,0:T(8,128)} custom-call(bf16[2,256,768]{2,1,0:T(8,128)(2,1)} %constant.6.clone.wide_tab, bf16[2,256,384]{2,1,0:T(8,128)(2,1)} %constant.7.clone.narrow_tab, bf16[128,768]{1,0:T(8,128)(2,1)} %constant.8.clone.back_tab, f32[256,256]{1,0:T(8,128)} %bitcast.10, f32[256,256]{1,0:T(8,128)} %bitcast.11, ...), custom_call_target="tpu_custom_call" | custom-call | tf_op jit(solution)/shard_map/pallas_call | solution.py:524
  241.3 3.0 %copy.10 = f32[2,4,1,256,256]{4,3,2,1,0:T(8,128)} copy(f32[2,4,1,256,256]{4,3,2,1,0:T(8,128)} %bitcast.7) | data formatting | bytes 4194304

commit v4 on v3

--- a/solution.py
+++ b/solution.py
@@ -16,11 +16,12 @@
 AHEAD = 3
 FIRST = 4
 EARLY = 12
-READY = 3
-HOP = 4
+HOP = 3
 TURN = 4
-NEAR = 3
-SCREEN = 4
+BURST = 3
+QUICK = 0
+NEAR = 4
+SCREEN = 6
 CORES = 2
 PART = 64
 SLOTS = 4
@@ -429,10 +430,6 @@
             def _():
                 body(k, v // 2)
 
-    def at(v, body):
-        ready = jnp.logical_and(v >= 0, v < 2 * stages)
-        pl.when(jnp.logical_and(ready, lax.rem(v, 2) == 0))(lambda: body(v // 2))
-
     def clear():
         half_buf[...] = jnp.zeros(half_buf.shape, jnp.float32)
         total_buf[...] = jnp.zeros(total_buf.shape, jnp.float32)
@@ -446,14 +443,19 @@
     each(0, early // 2, lambda q: mate_kind(1, q))
     clear()
     below = last - mine
-    settled = READY + HOP * jnp.maximum(mine, below)
-    turn = max(2 * stages - TURN, 0)
-
-    def turned(v, body):
-        steady = v >= 2 * turn - settled
-        q = jnp.where(steady, (v - settled) // 2, v - turn)
-        begun = jnp.where(steady, jnp.where(v >= settled, lax.rem(v - settled, 2) == 0, False), v >= turn)
-        pl.when(jnp.logical_and(begun, q < stages))(lambda: body(q))
+    hops = jnp.maximum(mine, below)
+    turn, quick = max(2 * stages - TURN, 0), max(stages - QUICK, 0)
+
+    def ready(v):
+        v = jnp.maximum(v, 0)
+        count = jnp.where(v // 2 > quick, v // 2, jnp.minimum((v + 1) // 2 - 1, quick))
+        return jnp.clip(count, 0, stages)
+
+    def crossing(v):
+        return jnp.minimum(ready(v - HOP * hops), jnp.maximum(v - turn + 1, 0) * BURST)
+
+    def newly(counter, v, body):
+        each(counter(v - 1), counter(v), body)
 
     def step(u):
         by_kind(u + AHEAD, first, send_kind)
@@ -462,15 +464,15 @@
         for half in range(1, width // LANES):
             pl.when(u == 0)(lambda: flip_half(half))
         pl.when(u == 1)(prepare)
-        at(u - READY, compute_stage)
-        at(u - READY - HOP * mine, lambda q: chain_stage(1, q))
-        at(u - READY - HOP * below, lambda q: chain_stage(0, q))
-        at(u - settled, final_stage)
-        turned(u, out_stage)
-        turned(u - NEAR, near_stage)
-        turned(u - NEAR - SCREEN, screen_stage)
-
-    length = max(2 * stages - 1 + READY + HOP * last, turn + stages)
+        newly(ready, u, compute_stage)
+        newly(ready, u - HOP * mine, lambda q: chain_stage(1, q))
+        newly(ready, u - HOP * below, lambda q: chain_stage(0, q))
+        newly(ready, u - HOP * hops, final_stage)
+        newly(crossing, u, out_stage)
+        newly(crossing, u - NEAR, near_stage)
+        newly(crossing, u - NEAR - SCREEN, screen_stage)
+
+    length = max(2 * stages + HOP * last, turn + stages // BURST) + 2
     each(0, length + NEAR + SCREEN, step)
 
     def finish(q):

time: 247 us -> 244 us (0.988)
  no operation moved by 1% of the time
where the time goes in v4:
time: 244 us; the launch traced here: 243 us
  Pallas kernels  240 us (98%)
  local copies, waits for them, and re-layouts  3.05 us (1%)
    pallas_call x1, Pallas kernels, local(): pl.pallas_call(functools.partial(screening_kernel, n, group, rows), out_s...  240 us

profile of v4, /device:TPU:21, one launch (start us, length us, event | category | flops | bytes accessed | tf_op | source)
XLA Modules:
  0.0 242.6 jit_solution(6555380393218900919)
XLA Ops:
  0.0 239.6 %shard_map.73 = f32[8,256,256]{2,1,0:T(8,128)} custom-call(bf16[2,256,768]{2,1,0:T(8,128)(2,1)} %constant.6.clone.wide_tab, bf16[2,256,384]{2,1,0:T(8,128)(2,1)} %constant.7.clone.narrow_tab, bf16[128,768]{1,0:T(8,128)(2,1)} %constant.8.clone.back_tab, f32[256,256]{1,0:T(8,128)} %bitcast.10, f32[256,256]{1,0:T(8,128)} %bitcast.11, ...), custom_call_target="tpu_custom_call" | custom-call | tf_op jit(solution)/shard_map/pallas_call | solution.py:526
  239.6 3.0 %copy.10 = f32[2,4,1,256,256]{4,3,2,1,0:T(8,128)} copy(f32[2,4,1,256,256]{4,3,2,1,0:T(8,128)} %bitcast.7) | data formatting | bytes 4194304
